TPU v7x, 32 devices: a whole 2x2x4 slice. The times are simulated.
32 devices in a mesh: row: 8 (over y, x, core), col: 4 (over z).
Axes of the slice: x: 2, y: 2, z: 4, core: 2. Of those that a mesh axis runs over, the one named last changes fastest.
Arguments:
- row_cells: int32 [3, 8192], P(None, 'row'), may hold values from 0 to 63
- col_cells: int32 [3, 32768], P(None, 'col'), may hold values from 0 to 63
- omega: float32 [16, 32768], P(None, 'col'), may hold values from -6 to 6
Outputs:
- basis: float32 [16, 8192], P(None, 'row')
- image: float32 [16, 32768], P(None, 'col')
- core: float32 [16, 16], replicated
All inputs are finite; a program needn't handle non-finite values.
Results may differ from a plain program's by a relative error of at most 0.0001.
Values sent between devices are 32-bit elements; how exact they have to be, the bound alone decides.
A program may use at most 64 MiB of HBM per device.

v0:
```python
import functools
import math

import jax
import jax.numpy as jnp
from jax import lax
from jax.experimental import pallas as pl
from jax.experimental.pallas import tpu as pltpu
from jax.sharding import PartitionSpec as P

BF16, F32 = jnp.bfloat16, jnp.float32
HIGHEST = lax.Precision.HIGHEST
NT = (((1,), (1,)), ((), ()))
NN = (((1,), (0,)), ((), ()))
LANES = 128
RATE = -math.log2(math.e) / 6.4


def split(x):
    high = x.astype(BF16)
    return high, (x - high.astype(F32)).astype(BF16)


def kernel(
    shape,
    row_ref, col_ref, omega_ref,
    basis_ref, image_ref, core_ref,
    rowb, colc, om, khi, klo,
    sk_src, sk_all, sk_hl, g_src, g_all, w_src, w_all, img, c_src, c_all, d_src, d_all,
    sk_ss, sk_rs, g_ss, g_rs, w_ss, w_rs, a_ss, a_rs, f_ss, f_rs, c_ss, c_rs, d_ss, d_rs,
):
    R, C, rank, M, N, chunk, wide, rows_total, order = shape
    me = lax.axis_index("row")
    mc = lax.axis_index("col")
    half = R // 2
    sib = me + 1 - 2 * lax.rem(me, 2)
    part = N // R
    chunks = M // chunk

    def row_of(t):
        return lax.rem(me + t, R)

    def row_from(t):
        return lax.rem(me - t + R, R)

    def remote(src, dst, ss, rs, axis, peer):
        return pltpu.make_async_remote_copy(
            src_ref=src, dst_ref=dst, send_sem=ss, recv_sem=rs,
            device_id={axis: peer}, device_id_type=pl.DeviceIdType.MESH,
        )

    barrier = pltpu.get_barrier_semaphore()
    for t in range(1, R):
        pl.semaphore_signal(barrier, inc=1, device_id={"row": row_of(t)}, device_id_type=pl.DeviceIdType.MESH)
    for t in range(1, C):
        pl.semaphore_signal(
            barrier, inc=1, device_id={"col": lax.rem(mc + t, C)}, device_id_type=pl.DeviceIdType.MESH
        )

    for d in range(3):
        rowb[d] = jnp.broadcast_to(row_ref[d : d + 1, :].astype(F32), (LANES, M)).T
    step = min(N, 1024)
    for s in range(N // step):
        cols = pl.ds(s * step, step)
        colc[0:3, cols] = col_ref[:, cols].astype(F32)
        high, low = split(0.25 * omega_ref[:, cols])
        om[0:rank, cols] = high
        om[rank : 2 * rank, cols] = low

    pl.semaphore_wait(barrier, R - 1 + C - 1)

    def sketch_copy(rc, t):
        return remote(
            sk_src.at[rc], sk_all.at[mc, rc], sk_ss.at[rc, t], sk_rs.at[rc, t], "col", lax.rem(mc + t, C)
        )

    def row_chunk(rc, carry):
        rows = pl.ds(pl.multiple_of(rc * chunk, chunk), chunk)

        def col_tile(ct, acc):
            cols = pl.ds(pl.multiple_of(ct * wide, wide), wide)
            repeat = (1, wide // LANES)
            sq = None
            for d in range(3):
                gap = jnp.tile(rowb[d, rows, :], repeat) - colc[d : d + 1, cols]
                sq = gap * gap if sq is None else sq + gap * gap
            sq = jnp.maximum(sq, 1e-30)
            value = jnp.exp2((sq * RATE) * lax.rsqrt(sq))
            high, low = split(value)
            khi[rows, cols] = high
            klo[rows, cols] = low
            o = om[:, cols]
            return (
                acc
                + lax.dot_general(o, high, NT, preferred_element_type=F32)
                + lax.dot_general(o, low, NT, preferred_element_type=F32)
            )

        acc = lax.fori_loop(0, N // wide, col_tile, jnp.zeros((2 * rank, chunk), F32))
        total = acc[:rank] + acc[rank:]
        sk_src[rc] = total
        sk_all[mc, rc] = total
        for t in range(1, C):
            sketch_copy(rc, t).start()
        return carry

    lax.fori_loop(0, chunks, row_chunk, 0)

    for rc in range(chunks):
        for t in range(1, C):
            sketch_copy(rc, t).wait_recv()
    pieces = []
    for rc in range(chunks):
        total = sk_all[0, rc]
        for c in range(1, C):
            total = total + sk_all[c, rc]
        pieces.append(total)
    sketch = jnp.concatenate(pieces, axis=1)
    high, low = split(0.25 * sketch)
    sk_hl[0:rank, :] = high
    sk_hl[rank : 2 * rank, :] = low
    gram = lax.dot_general(sketch, sketch, NT, precision=HIGHEST, preferred_element_type=F32) / rows_total
    g_src[...] = jnp.zeros_like(g_src)
    g_src[:, rank : 2 * rank] = gram
    g_all[me] = g_src[...]

    def gram_copy(t):
        return remote(g_src, g_all.at[me], g_ss.at[t], g_rs.at[t], "row", row_of(t))

    for t in range(1, R):
        gram_copy(t).start()

    def w_copy(t):
        return remote(w_src.at[t], w_all.at[me], w_ss.at[t], w_rs.at[t], "row", row_of(t))

    def product(peer):
        cols = pl.ds(pl.multiple_of(peer * part, part), part)
        s = sk_hl[...]
        acc = lax.dot_general(s, khi[:, cols], NN, preferred_element_type=F32)
        acc = acc + lax.dot_general(s, klo[:, cols], NN, preferred_element_type=F32)
        return acc[:rank] + acc[rank:]

    def block(t, carry):
        w_src[t] = product(row_of(t))
        w_copy(t).start()
        return carry

    lax.fori_loop(1, R, block, 0)
    w_all[me] = product(me)

    for t in range(1, R):
        gram_copy(t).wait_recv()
    mat = g_all[0]
    for r in range(1, R):
        mat = mat + g_all[r]
    sub = lax.broadcasted_iota(jnp.int32, mat.shape, 0)
    lane = lax.broadcasted_iota(jnp.int32, mat.shape, 1)
    mat = mat + jnp.where(lane == sub, 1.0, 0.0)
    for k in range(rank - 1):
        row = mat[k : k + 1, :]
        factor = mat[:, rank + k : rank + k + 1] * (1.0 / mat[k : k + 1, rank + k : rank + k + 1])
        mat = mat - jnp.where(sub > k, factor * row, 0.0)
    diag = jnp.sum(jnp.where(lane == sub + rank, mat, 0.0), axis=1, keepdims=True)
    inverse = (mat * (1.0 / jnp.sqrt(diag)))[:, :rank]
    inverse = jnp.where(lane[:, :rank] <= sub[:, :rank], inverse, 0.0)
    basis_ref[...] = jnp.dot(inverse, sketch, precision=HIGHEST, preferred_element_type=F32)

    for t in range(1, R):
        w_copy(t).wait_recv()
    total = w_all[0]
    for r in range(1, R):
        total = total + w_all[r]
    mine = jnp.dot(inverse, total, precision=HIGHEST, preferred_element_type=F32)
    img[me] = mine

    def far_copy(t):
        return remote(img.at[me], img.at[me], a_ss.at[t], a_rs.at[t], "row", row_of(2 * t))

    def near_copy(t):
        slot = row_from(2 * t)
        return remote(img.at[slot], img.at[slot], f_ss.at[t], f_rs.at[t], "row", sib)

    def core_copy(t):
        return remote(c_src, c_all.at[me], c_ss.at[t], c_rs.at[t], "row", row_of(t))

    def last_copy(t):
        return remote(d_src, d_all.at[mc], d_ss.at[t], d_rs.at[t], "col", lax.rem(mc + t, C))

    core = lax.dot_general(mine, mine, NT, precision=HIGHEST, preferred_element_type=F32) / order
    c_src[...] = jnp.zeros_like(c_src)
    c_src[:, 0:rank] = core
    c_all[me] = c_src[...]
    for t in range(1, R):
        core_copy(t).start()
    for t in range(half - 1, 0, -1):
        far_copy(t).start()
    near_copy(0).start()
    for t in range(1, R):
        core_copy(t).wait_recv()
    core = c_all[0]
    for r in range(1, R):
        core = core + c_all[r]
    d_src[...] = core
    d_all[mc] = core
    for t in range(1, C):
        last_copy(t).start()
    for t in range(1, half):
        far_copy(t).wait_recv()
        near_copy(t).start()
    for t in range(half):
        near_copy(t).wait_recv()
    for r in range(R):
        image_ref[:, r * part : (r + 1) * part] = img[r]
    for t in range(1, C):
        last_copy(t).wait_recv()
    core = d_all[0]
    for c in range(1, C):
        core = core + d_all[c]
    core_ref[...] = core[:, 0:rank]

    for rc in range(chunks):
        for t in range(1, C):
            sketch_copy(rc, t).wait_send()
    for t in range(1, R):
        gram_copy(t).wait_send()
        w_copy(t).wait_send()
        core_copy(t).wait_send()
    for t in range(1, half):
        far_copy(t).wait_send()
    for t in range(half):
        near_copy(t).wait_send()
    for t in range(1, C):
        last_copy(t).wait_send()


def finish(*refs):
    for source, target in zip(refs[:3], refs[3:]):
        target[...] = source[...]


def shards(row_cells, col_cells, omega):
    R, C = lax.axis_size("row"), lax.axis_size("col")
    rank = omega.shape[0]
    M, N = row_cells.shape[1], col_cells.shape[1]
    chunk, wide = min(M, 256), min(N, 1024)
    chunks, part = M // chunk, N // R
    shape = (R, C, rank, M, N, chunk, wide, M * R, N * C)
    vmem = pltpu.VMEM
    dma = pltpu.SemaphoreType.DMA
    full = pl.BlockSpec(memory_space=pltpu.VMEM)
    out_shape = (
        jax.ShapeDtypeStruct((rank, M), F32),
        jax.ShapeDtypeStruct((rank, N), F32),
        jax.ShapeDtypeStruct((rank, rank), F32),
    )
    outs = pl.pallas_call(
        functools.partial(kernel, shape),
        out_shape=out_shape,
        in_specs=[full] * 3,
        out_specs=(full,) * 3,
        scratch_shapes=[
            vmem((3, M, LANES), F32),
            vmem((8, N), F32),
            vmem((2 * rank, N), BF16),
            vmem((M, N), BF16),
            vmem((M, N), BF16),
            vmem((chunks, rank, chunk), F32),
            vmem((C, chunks, rank, chunk), F32),
            vmem((2 * rank, M), BF16),
            vmem((rank, LANES), F32),
            vmem((R, rank, LANES), F32),
            vmem((R, rank, part), F32),
            vmem((R, rank, part), F32),
            vmem((R, rank, part), F32),
            vmem((rank, LANES), F32),
            vmem((R, rank, LANES), F32),
            vmem((rank, LANES), F32),
            vmem((C, rank, LANES), F32),
            dma((chunks, C)), dma((chunks, C)),
            dma((R,)), dma((R,)),
            dma((R,)), dma((R,)),
            dma((R,)), dma((R,)),
            dma((R,)), dma((R,)),
            dma((R,)), dma((R,)),
            dma((C,)), dma((C,)),
        ],
        compiler_params=pltpu.CompilerParams(
            collective_id=0, has_side_effects=True, vmem_limit_bytes=46 * 1024 * 1024
        ),
    )(row_cells, col_cells, omega)
    return pl.pallas_call(
        finish,
        out_shape=out_shape,
        in_specs=[full] * 3,
        out_specs=(full,) * 3,
        compiler_params=pltpu.CompilerParams(vmem_limit_bytes=4 * 1024 * 1024),
    )(*outs)


def solution(mesh):
    return jax.shard_map(
        shards,
        mesh=mesh,
        in_specs=(P(None, "row"), P(None, "col"), P(None, "col")),
        out_specs=(P(None, "row"), P(None, "col"), P()),
        check_vma=False,
    )
```

profile of v0, /device:TPU:0, one launch (start us, length us, event | category | flops | bytes accessed | tf_op | source)
XLA Modules:
  0.0 54.4 jit_solution(16260776731345281092)
XLA Ops:
  0.6 0.0 copy-start
  0.6 1.0 %copy-done = f32[16,8192]{1,0:T(8,128)S(1)} copy-done((f32[16,8192]{1,0:T(8,128)S(1)}, f32[16,8192]{1,0:T(8,128)}, u32[]{:S(2)}) %copy-start) | copy-done | bytes 524312
  1.7 0.0 copy-start.1
  1.7 0.9 %copy-done.1 = s32[3,8192]{1,0:T(4,128)S(1)} copy-done((s32[3,8192]{1,0:T(4,128)S(1)}, s32[3,8192]{1,0:T(4,128)}, u32[]{:S(2)}) %copy-start.1) | copy-done | bytes 98328
  2.6 0.0 copy-start.2
  2.6 0.7 %copy-done.2 = s32[3,1024]{1,0:T(4,128)S(1)} copy-done((s32[3,1024]{1,0:T(4,128)S(1)}, s32[3,1024]{1,0:T(4,128)}, u32[]{:S(2)}) %copy-start.2) | copy-done | bytes 12312
  3.3 50.2 %shard_map.58 = (f32[16,1024]{1,0:T(8,128)S(1)}, f32[16,8192]{1,0:T(8,128)S(1)}, f32[16,16]{1,0:T(8,128)S(1)}) custom-call(s32[3,1024]{1,0:T(4,128)S(1)} %copy-done.2, s32[3,8192]{1,0:T(4,128)S(1)} %copy-done.1, f32[16,8192]{1,0:T(8,128)S(1)} %copy-done), custom_call_target="tpu_custom_call" | custom-call | tf_op jit(solution)/shard_map/pallas_call | solution.py:256
  53.5 0.8 %shard_map.59 = (f32[16,1024]{1,0:T(8,128)}, f32[16,8192]{1,0:T(8,128)}, f32[16,16]{1,0:T(8,128)}) custom-call(f32[16,1024]{1,0:T(8,128)S(1)} %get-tuple-element.6.refs_0_, f32[16,8192]{1,0:T(8,128)S(1)} %get-tuple-element.7.refs_1_, f32[16,16]{1,0:T(8,128)S(1)} %get-tuple-element.8.refs_2_), custom_call_target="tpu_custom_call" | custom-call | tf_op jit(solution)/shard_map/pallas_call | solution.py:291
Async XLA Ops:
  0.6 1.0 %copy-start = (f32[16,8192]{1,0:T(8,128)S(1)}, f32[16,8192]{1,0:T(8,128)}, u32[]{:S(2)}) copy-start(f32[16,8192]{1,0:T(8,128)} %omega_ref.1) | copy-start | bytes 1572868
  1.7 0.9 %copy-start.1 = (s32[3,8192]{1,0:T(4,128)S(1)}, s32[3,8192]{1,0:T(4,128)}, u32[]{:S(2)}) copy-start(s32[3,8192]{1,0:T(4,128)} %col_ref.1) | copy-start | bytes 294916
  2.6 0.7 %copy-start.2 = (s32[3,1024]{1,0:T(4,128)S(1)}, s32[3,1024]{1,0:T(4,128)}, u32[]{:S(2)}) copy-start(s32[3,1024]{1,0:T(4,128)} %row_ref.1) | copy-start | bytes 36868
where the time goes:
time: 54.6 us; the launch traced here: 54.4 us
  Pallas kernels  51.1 us (94%)
  local copies, waits for them, and re-layouts  2.66 us (5%)
  between operations  0.65 us (1%)
    pallas_call x1, Pallas kernels, shards(): pl.pallas_call(functools.partial(kernel, shape), out_shape=out_shape, in_...  50.2 us
    unnamed x6, local copies, waits for them, and re-layouts  2.66 us

commit v1 on v0

v1 whole, which is shorter than its diff:
```python
import functools
import math

import jax
import jax.numpy as jnp
from jax import lax
from jax.experimental import pallas as pl
from jax.experimental.pallas import tpu as pltpu
from jax.sharding import PartitionSpec as P

BF16, F32 = jnp.bfloat16, jnp.float32
HIGHEST = lax.Precision.HIGHEST
NT = (((1,), (1,)), ((), ()))
NN = (((1,), (0,)), ((), ()))
LANES = 128
RATE = -math.log2(math.e) / 6.4
UNIT = 256
LEAD = 3
BUFS = 4
SLICE = 64


def split(x):
    high = x.astype(BF16)
    return high, (x - high.astype(F32)).astype(BF16)


def features(cells, left):
    x = [cells[d : d + 1, :].astype(F32) - 32.0 for d in range(3)]
    norm = x[0] * x[0] + x[1] * x[1] + x[2] * x[2]
    high = jnp.floor(norm * 0.0625) * 16.0
    low = norm - high
    one, zero = jnp.ones_like(norm), jnp.zeros_like(norm)
    if left:
        rows = [-2.0 * x[0], -2.0 * x[1], -2.0 * x[2], one, one, high, low, zero]
    else:
        rows = [x[0], x[1], x[2], high, low, one, one, zero]
    return jnp.concatenate(rows, axis=0)


def kernel(
    shape,
    row_hbm, col_hbm, omega_hbm,
    basis_ref, image_ref, core_ref,
    row_in, col_in, om_in, rowf, colf, om, khi, klo, sq0, sq1, sq2, sq3, hi0, hi1, lo0, lo1,
    sk_src, sk_all, sk_hl, g_src, g_all, wp, s_in, w_src, w_all, img, c_src, c_all, d_src, d_all,
    in_s, sk_ss, sk_rs, g_ss, g_rs, p_ss, p_rs, w_ss, w_rs, a_ss, a_rs, f_ss, f_rs, c_ss, c_rs, d_ss, d_rs,
):
    R, C, rank, M, N, rows_total, order = shape
    me = lax.axis_index("row")
    mc = lax.axis_index("col")
    half = R // 2
    side = lax.rem(me, 2)
    chip = me // 2
    sib = me + 1 - 2 * side
    part = N // R
    chunk = min(M, UNIT)
    chunks = M // chunk
    units = N // UNIT
    sq = (sq0, sq1, sq2, sq3)
    hi, lo = (hi0, hi1), (lo0, lo1)
    binary = half & (half - 1) == 0
    far_first = sorted(range(1, half), key=lambda t: -bin(t).count("1"))

    def row_of(t):
        return lax.rem(me + t, R)

    def chip_to(t):
        if not binary:
            return lax.rem(chip + t, half)
        total, bit = 0, 1
        while bit < half:
            total = total + bit * lax.rem(chip // bit + t // bit, 2)
            bit *= 2
        return total

    def chip_from(t):
        return chip_to(t) if binary else lax.rem(chip + half - t, half)

    def remote(src, dst, ss, rs, axis, peer):
        return pltpu.make_async_remote_copy(
            src_ref=src, dst_ref=dst, send_sem=ss, recv_sem=rs,
            device_id={axis: peer}, device_id_type=pl.DeviceIdType.MESH,
        )

    loads = [
        pltpu.make_async_copy(source, target, in_s.at[i])
        for i, (source, target) in enumerate(((col_hbm, col_in), (row_hbm, row_in), (omega_hbm, om_in)))
    ]
    for load in loads:
        load.start()
    barrier = pltpu.get_barrier_semaphore()
    for t in range(1, R):
        pl.semaphore_signal(barrier, inc=1, device_id={"row": row_of(t)}, device_id_type=pl.DeviceIdType.MESH)
    for t in range(1, C):
        pl.semaphore_signal(
            barrier, inc=1, device_id={"col": lax.rem(mc + t, C)}, device_id_type=pl.DeviceIdType.MESH
        )

    loads[0].wait()
    loads[1].wait()
    rowf[0:8, :] = features(row_in[...], False).astype(BF16)
    rowf[8:16, :] = jnp.zeros((8, M), BF16)
    step = min(N, 1024)
    for s in range(N // step):
        left = features(col_in[:, s * step : (s + 1) * step], True)
        for b in range(step // LANES):
            block = jnp.concatenate(
                [left[:, b * LANES : (b + 1) * LANES], jnp.zeros((LANES - 8, LANES), F32)], axis=0
            )
            colf[s * step + b * LANES : s * step + (b + 1) * LANES, :] = block.T.astype(BF16)
    loads[2].wait()
    for s in range(N // step):
        cols = pl.ds(s * step, step)
        high, low = split(0.25 * om_in[:, cols])
        om[0:rank, cols] = high
        om[rank : 2 * rank, cols] = low

    def sketch_copy(rc, t):
        return remote(
            sk_src.at[rc], sk_all.at[mc, rc], sk_ss.at[rc, t], sk_rs.at[rc, t], "col", lax.rem(mc + t, C)
        )

    def squared(u, right):
        return lax.dot_general(
            colf[u * UNIT : (u + 1) * UNIT, 0:16], right, NN, preferred_element_type=F32
        )

    for u in range(LEAD):
        sq[u][...] = squared(u, rowf[:, 0:chunk])

    def row_chunk(rc, carry):
        start = pl.multiple_of(rc * chunk, chunk)
        right = rowf[:, pl.ds(start, chunk)]
        right_next = rowf[:, pl.ds(pl.multiple_of(lax.rem(rc + 1, chunks) * chunk, chunk), chunk)]

        def use(u, acc):
            o = om[:, u * UNIT : (u + 1) * UNIT]
            for stage, whole in ((hi, khi), (lo, klo)):
                tile = jnp.concatenate([stage[u % 2][q] for q in range(chunk // LANES)], axis=1)
                acc = acc + lax.dot_general(o, tile, NN, preferred_element_type=F32)
                for q in range(chunk // LANES):
                    for p in range(UNIT // LANES):
                        whole[u * (UNIT // LANES) + p, pl.ds(start + q * LANES, LANES), :] = (
                            stage[u % 2][q, p * LANES : (p + 1) * LANES, :].T
                        )
            return acc

        acc = jnp.zeros((2 * rank, chunk), F32)
        for u in range(units):
            ahead = u + LEAD
            sq[ahead % BUFS][...] = squared(ahead % units, right if ahead < units else right_next)
            if u > 0:
                acc = use(u - 1, acc)
            for s in range(UNIT // SLICE):
                rows = slice(s * SLICE, (s + 1) * SLICE)
                value = jnp.maximum(sq[u % BUFS][rows, :], 1e-30)
                value = jnp.exp2((value * RATE) * lax.rsqrt(value))
                high, low = split(value)
                for q in range(chunk // LANES):
                    hi[u % 2][q, rows, :] = high[:, q * LANES : (q + 1) * LANES]
                    lo[u % 2][q, rows, :] = low[:, q * LANES : (q + 1) * LANES]
        acc = use(units - 1, acc)
        total = acc[:rank] + acc[rank:]

        @pl.when(rc == 0)
        def _():
            pl.semaphore_wait(barrier, R - 1 + C - 1)

        sk_src[rc] = total
        sk_all[mc, rc] = total
        for t in range(1, C):
            sketch_copy(rc, t).start()
        return carry

    lax.fori_loop(0, chunks, row_chunk, 0)

    for rc in range(chunks):
        for t in range(1, C):
            sketch_copy(rc, t).wait_recv()
    pieces = []
    for rc in range(chunks):
        total = sk_all[0, rc]
        for c in range(1, C):
            total = total + sk_all[c, rc]
        pieces.append(total)
    sketch = jnp.concatenate(pieces, axis=1)
    high, low = split(0.25 * sketch)
    sk_hl[0:rank, :] = high
    sk_hl[rank : 2 * rank, :] = low
    gram = lax.dot_general(sketch, sketch, NT, precision=HIGHEST, preferred_element_type=F32) / rows_total
    g_src[...] = jnp.zeros_like(g_src)
    g_src[:, rank : 2 * rank] = gram
    g_all[me] = g_src[...]

    def gram_copy(t):
        return remote(g_src, g_all.at[me], g_ss.at[t], g_rs.at[t], "row", row_of(t))

    for t in range(1, R):
        gram_copy(t).start()

    def pair_copy(t):
        return remote(wp.at[t, 1 - side], s_in.at[t], p_ss.at[t], p_rs.at[t], "row", sib)

    def w_copy(t):
        return remote(w_src.at[t], w_all.at[t], w_ss.at[t], w_rs.at[t], "row", 2 * chip_to(t) + side)

    tiles = 2 * part // LANES

    def product(t):
        base = chip_to(t) * tiles
        s = sk_hl[...]
        acc = None
        for whole in (khi, klo):
            block = jnp.concatenate([whole[base + i] for i in range(tiles)], axis=1)
            term = lax.dot_general(s, block, NN, preferred_element_type=F32)
            acc = term if acc is None else acc + term
        acc = acc[:rank] + acc[rank:]
        wp[t, 0] = acc[:, :part]
        wp[t, 1] = acc[:, part:]

    def forward(t):
        pair_copy(t).wait_recv()
        w_src[t] = wp[t, side] + s_in[t]
        w_copy(t).start()

    before = None
    for t in far_first:
        product(t)
        pair_copy(t).start()
        if before is not None:
            forward(before)
        before = t
    for t in range(1, R):
        gram_copy(t).wait_recv()
    product(0)
    mat = g_all[0]
    for r in range(1, R):
        mat = mat + g_all[r]
    sub = lax.broadcasted_iota(jnp.int32, mat.shape, 0)
    lane = lax.broadcasted_iota(jnp.int32, mat.shape, 1)
    mat = mat + jnp.where(lane == sub, 1.0, 0.0)
    for k in range(rank - 1):
        row = mat[k : k + 1, :]
        factor = mat[:, rank + k : rank + k + 1] * (1.0 / mat[k : k + 1, rank + k : rank + k + 1])
        mat = mat - jnp.where(sub > k, factor * row, 0.0)
    diag = jnp.sum(jnp.where(lane == sub + rank, mat, 0.0), axis=1, keepdims=True)
    inverse = (mat * (1.0 / jnp.sqrt(diag)))[:, :rank]
    inverse = jnp.where(lane[:, :rank] <= sub[:, :rank], inverse, 0.0)
    pair_copy(0).start()
    if before is not None:
        forward(before)
    basis_ref[...] = jnp.dot(inverse, sketch, precision=HIGHEST, preferred_element_type=F32)
    pair_copy(0).wait_recv()
    total = wp[0, side] + s_in[0]
    for t in far_first:
        w_copy(t).wait_recv()
        total = total + w_all[t]
    mine = jnp.dot(inverse, total, precision=HIGHEST, preferred_element_type=F32)
    img[me] = mine

    def far_copy(t):
        return remote(img.at[me], img.at[me], a_ss.at[t], a_rs.at[t], "row", 2 * chip_to(t) + side)

    def near_copy(t):
        slot = 2 * chip_from(t) + side
        return remote(img.at[slot], img.at[slot], f_ss.at[t], f_rs.at[t], "row", sib)

    def core_copy(t):
        return remote(c_src, c_all.at[me], c_ss.at[t], c_rs.at[t], "row", row_of(t))

    def last_copy(t):
        return remote(d_src, d_all.at[mc], d_ss.at[t], d_rs.at[t], "col", lax.rem(mc + t, C))

    core = lax.dot_general(mine, mine, NT, precision=HIGHEST, preferred_element_type=F32) / order
    c_src[...] = jnp.zeros_like(c_src)
    c_src[:, 0:rank] = core
    c_all[me] = c_src[...]
    for t in range(1, R):
        core_copy(t).start()
    for t in far_first:
        far_copy(t).start()
    near_copy(0).start()
    for t in range(1, R):
        core_copy(t).wait_recv()
    core = c_all[0]
    for r in range(1, R):
        core = core + c_all[r]
    d_src[...] = core
    d_all[mc] = core
    for t in range(1, C):
        last_copy(t).start()
    for t in reversed(far_first):
        far_copy(t).wait_recv()
        near_copy(t).start()
    for t in range(half):
        near_copy(t).wait_recv()
    for r in range(R):
        image_ref[:, r * part : (r + 1) * part] = img[r]
    for t in range(1, C):
        last_copy(t).wait_recv()
    core = d_all[0]
    for c in range(1, C):
        core = core + d_all[c]
    core_ref[...] = core[:, 0:rank]

    for rc in range(chunks):
        for t in range(1, C):
            sketch_copy(rc, t).wait_send()
    for t in range(1, R):
        gram_copy(t).wait_send()
        core_copy(t).wait_send()
    for t in range(half):
        pair_copy(t).wait_send()
        near_copy(t).wait_send()
    for t in far_first:
        w_copy(t).wait_send()
        far_copy(t).wait_send()
    for t in range(1, C):
        last_copy(t).wait_send()


def finish(*refs):
    copies = [pltpu.make_async_copy(refs[i], refs[3 + i], refs[6].at[i]) for i in range(3)]
    for copy in copies:
        copy.start()
    for copy in copies:
        copy.wait()


def shards(row_cells, col_cells, omega):
    R, C = lax.axis_size("row"), lax.axis_size("col")
    rank = omega.shape[0]
    M, N = row_cells.shape[1], col_cells.shape[1]
    chunk = min(M, UNIT)
    chunks, part, half = M // chunk, N // R, R // 2
    shape = (R, C, rank, M, N, M * R, N * C)
    vmem = pltpu.VMEM
    dma = pltpu.SemaphoreType.DMA
    full = pl.BlockSpec(memory_space=pltpu.VMEM)
    hbm = pl.BlockSpec(memory_space=pltpu.HBM)
    out_shape = (
        jax.ShapeDtypeStruct((rank, M), F32),
        jax.ShapeDtypeStruct((rank, N), F32),
        jax.ShapeDtypeStruct((rank, rank), F32),
    )
    outs = pl.pallas_call(
        functools.partial(kernel, shape),
        out_shape=out_shape,
        in_specs=[hbm] * 3,
        out_specs=(full,) * 3,
        scratch_shapes=[
            vmem(row_cells.shape, jnp.int32),
            vmem(col_cells.shape, jnp.int32),
            vmem((rank, N), F32),
            vmem((16, M), BF16),
            vmem((N, LANES), BF16),
            vmem((2 * rank, N), BF16),
            vmem((N // LANES, M, LANES), BF16),
            vmem((N // LANES, M, LANES), BF16),
            *[vmem((UNIT, chunk), F32)] * BUFS,
            *[vmem((chunk // LANES, UNIT, LANES), BF16)] * 4,
            vmem((chunks, rank, chunk), F32),
            vmem((C, chunks, rank, chunk), F32),
            vmem((2 * rank, M), BF16),
            vmem((rank, LANES), F32),
            vmem((R, rank, LANES), F32),
            vmem((half, 2, rank, part), F32),
            vmem((half, rank, part), F32),
            vmem((half, rank, part), F32),
            vmem((half, rank, part), F32),
            vmem((R, rank, part), F32),
            vmem((rank, LANES), F32),
            vmem((R, rank, LANES), F32),
            vmem((rank, LANES), F32),
            vmem((C, rank, LANES), F32),
            dma((3,)),
            dma((chunks, C)), dma((chunks, C)),
            dma((R,)), dma((R,)),
            dma((half,)), dma((half,)),
            dma((half,)), dma((half,)),
            dma((half,)), dma((half,)),
            dma((half,)), dma((half,)),
            dma((R,)), dma((R,)),
            dma((C,)), dma((C,)),
        ],
        compiler_params=pltpu.CompilerParams(
            collective_id=0, has_side_effects=True, vmem_limit_bytes=48 * 1024 * 1024
        ),
    )(row_cells, col_cells, omega)
    return pl.pallas_call(
        finish,
        out_shape=out_shape,
        in_specs=[full] * 3,
        out_specs=(hbm,) * 3,
        scratch_shapes=[dma((3,))],
        compiler_params=pltpu.CompilerParams(vmem_limit_bytes=4 * 1024 * 1024),
    )(*outs)


def solution(mesh):
    return jax.shard_map(
        shards,
        mesh=mesh,
        in_specs=(P(None, "row"), P(None, "col"), P(None, "col")),
        out_specs=(P(None, "row"), P(None, "col"), P()),
        check_vma=False,
    )
```

time: 54.6 us -> 44.2 us (0.81)
  Pallas kernels: 51.1 us -> 40.7 us
    pallas_call x1, Pallas kernels: 50.2 us -> 39.8 us  [shards(): pl.pallas_call(functools.partial(kernel, shape), out_shape=out_shape, in_...]
where the time goes in v1:
time: 44.2 us; the launch traced here: 44 us
  Pallas kernels  40.7 us (92%)
  local copies, waits for them, and re-layouts  2.66 us (6%)
  between operations  0.65 us (1%)
    pallas_call x1, Pallas kernels, shards(): pl.pallas_call(functools.partial(kernel, shape), out_shape=out_shape, in_...  39.8 us
    unnamed x6, local copies, waits for them, and re-layouts  2.66 us

profile of v1, /device:TPU:0, one launch (start us, length us, event | category | flops | bytes accessed | tf_op | source)
XLA Modules:
  0.0 44.0 jit_solution(15316098800246006468)
XLA Ops:
  0.6 0.0 copy-start
  0.6 1.0 %copy-done = f32[16,8192]{1,0:T(8,128)S(1)} copy-done((f32[16,8192]{1,0:T(8,128)S(1)}, f32[16,8192]{1,0:T(8,128)}, u32[]{:S(2)}) %copy-start) | copy-done | bytes 524312
  1.7 0.0 copy-start.1
  1.7 0.9 %copy-done.1 = s32[3,8192]{1,0:T(4,128)S(1)} copy-done((s32[3,8192]{1,0:T(4,128)S(1)}, s32[3,8192]{1,0:T(4,128)}, u32[]{:S(2)}) %copy-start.1) | copy-done | bytes 98328
  2.6 0.0 copy-start.2
  2.6 0.7 %copy-done.2 = s32[3,1024]{1,0:T(4,128)S(1)} copy-done((s32[3,1024]{1,0:T(4,128)S(1)}, s32[3,1024]{1,0:T(4,128)}, u32[]{:S(2)}) %copy-start.2) | copy-done | bytes 12312
  3.3 39.8 %shard_map.58 = (f32[16,1024]{1,0:T(8,128)S(1)}, f32[16,8192]{1,0:T(8,128)S(1)}, f32[16,16]{1,0:T(8,128)S(1)}) custom-call(s32[3,1024]{1,0:T(4,128)S(1)} %copy-done.2, s32[3,8192]{1,0:T(4,128)S(1)} %copy-done.1, f32[16,8192]{1,0:T(8,128)S(1)} %copy-done), custom_call_target="tpu_custom_call" | custom-call | tf_op jit(solution)/shard_map/pallas_call | solution.py:347
  43.1 0.8 %shard_map.59 = (f32[16,1024]{1,0:T(8,128)}, f32[16,8192]{1,0:T(8,128)}, f32[16,16]{1,0:T(8,128)}) custom-call(f32[16,1024]{1,0:T(8,128)S(1)} %get-tuple-element.6.refs_0_, f32[16,8192]{1,0:T(8,128)S(1)} %get-tuple-element.7.refs_1_, f32[16,16]{1,0:T(8,128)S(1)} %get-tuple-element.8.refs_2_), custom_call_target="tpu_custom_call" | custom-call | tf_op jit(solution)/shard_map/pallas_call | solution.py:391
Async XLA Ops:
  0.6 1.0 %copy-start = (f32[16,8192]{1,0:T(8,128)S(1)}, f32[16,8192]{1,0:T(8,128)}, u32[]{:S(2)}) copy-start(f32[16,8192]{1,0:T(8,128)} %omega_hbm.1) | copy-start | bytes 1572868
  1.7 0.9 %copy-start.1 = (s32[3,8192]{1,0:T(4,128)S(1)}, s32[3,8192]{1,0:T(4,128)}, u32[]{:S(2)}) copy-start(s32[3,8192]{1,0:T(4,128)} %col_hbm.1) | copy-start | bytes 294916
  2.6 0.7 %copy-start.2 = (s32[3,1024]{1,0:T(4,128)S(1)}, s32[3,1024]{1,0:T(4,128)}, u32[]{:S(2)}) copy-start(s32[3,1024]{1,0:T(4,128)} %row_hbm.1) | copy-start | bytes 36868

commit v2 on v1

--- a/solution.py
+++ b/solution.py
@@ -18,11 +18,20 @@
 LEAD = 3
 BUFS = 4
 SLICE = 64
+VMEM_LIMIT = 48000 * 1024
 
 
 def split(x):
     high = x.astype(BF16)
     return high, (x - high.astype(F32)).astype(BF16)
+
+
+def loop(first, last, body):
+    if last - first < 64:
+        for k in range(first, last):
+            body(k, 0)
+    else:
+        lax.fori_loop(first, last, body, 0)
 
 
 def features(cells, left):
@@ -43,8 +52,8 @@
     row_hbm, col_hbm, omega_hbm,
     basis_ref, image_ref, core_ref,
     row_in, col_in, om_in, rowf, colf, om, khi, klo, sq0, sq1, sq2, sq3, hi0, hi1, lo0, lo1,
-    sk_src, sk_all, sk_hl, g_src, g_all, wp, s_in, w_src, w_all, img, c_src, c_all, d_src, d_all,
-    in_s, sk_ss, sk_rs, g_ss, g_rs, p_ss, p_rs, w_ss, w_rs, a_ss, a_rs, f_ss, f_rs, c_ss, c_rs, d_ss, d_rs,
+    sk_src, sk_all, sk_hl, g_src, g_all, wacc, wp, s_in, w_src, w_all, img, c_src, c_all,
+    in_s, sk_rs, p_rs, a_rs, one_s,
 ):
     R, C, rank, M, N, rows_total, order = shape
     me = lax.axis_index("row")
@@ -56,6 +65,10 @@
     part = N // R
     chunk = min(M, UNIT)
     chunks = M // chunk
+    group = max(chunks // 2, 1)
+    groups = chunks // group
+    devices = R * C
+    index = mc * R + me
     units = N // UNIT
     sq = (sq0, sq1, sq2, sq3)
     hi, lo = (hi0, hi1), (lo0, lo1)
@@ -83,6 +96,14 @@
             device_id={axis: peer}, device_id_type=pl.DeviceIdType.MESH,
         )
 
+    sk_ss, g_ss, g_rs, p_ss, w_ss, w_rs, a_ss, f_ss, f_rs, c_ss, c_rs = (one_s.at[i] for i in range(11))
+
+    def all_sent(ref, ss):
+        remote(ref, ref, ss, ss, "row", sib).wait_send()
+
+    def all_received(ref, rs):
+        remote(ref, ref, rs, rs, "row", sib).wait_recv()
+
     loads = [
         pltpu.make_async_copy(source, target, in_s.at[i])
         for i, (source, target) in enumerate(((col_hbm, col_in), (row_hbm, row_in), (omega_hbm, om_in)))
@@ -90,12 +111,16 @@
     for load in loads:
         load.start()
     barrier = pltpu.get_barrier_semaphore()
-    for t in range(1, R):
-        pl.semaphore_signal(barrier, inc=1, device_id={"row": row_of(t)}, device_id_type=pl.DeviceIdType.MESH)
-    for t in range(1, C):
-        pl.semaphore_signal(
-            barrier, inc=1, device_id={"col": lax.rem(mc + t, C)}, device_id_type=pl.DeviceIdType.MESH
-        )
+
+    def peer(k):
+        other = lax.rem(index + k, devices)
+        return {"row": lax.rem(other, R), "col": other // R}
+
+    def greet(k, carry):
+        pl.semaphore_signal(barrier, inc=1, device_id=peer(k), device_id_type=pl.DeviceIdType.MESH)
+        return carry
+
+    loop(1, devices, greet)
 
     loads[0].wait()
     loads[1].wait()
@@ -118,7 +143,7 @@
 
     def sketch_copy(rc, t):
         return remote(
-            sk_src.at[rc], sk_all.at[mc, rc], sk_ss.at[rc, t], sk_rs.at[rc, t], "col", lax.rem(mc + t, C)
+            sk_src.at[rc], sk_all.at[mc, rc], sk_ss, sk_rs.at[rc // group], "col", lax.rem(mc + t, C)
         )
 
     def squared(u, right):
@@ -165,7 +190,7 @@
 
         @pl.when(rc == 0)
         def _():
-            pl.semaphore_wait(barrier, R - 1 + C - 1)
+            pl.semaphore_wait(barrier, devices - 1)
 
         sk_src[rc] = total
         sk_all[mc, rc] = total
@@ -175,47 +200,72 @@
 
     lax.fori_loop(0, chunks, row_chunk, 0)
 
-    for rc in range(chunks):
-        for t in range(1, C):
-            sketch_copy(rc, t).wait_recv()
-    pieces = []
-    for rc in range(chunks):
-        total = sk_all[0, rc]
-        for c in range(1, C):
-            total = total + sk_all[c, rc]
-        pieces.append(total)
-    sketch = jnp.concatenate(pieces, axis=1)
-    high, low = split(0.25 * sketch)
-    sk_hl[0:rank, :] = high
-    sk_hl[rank : 2 * rank, :] = low
-    gram = lax.dot_general(sketch, sketch, NT, precision=HIGHEST, preferred_element_type=F32) / rows_total
+    tiles = 2 * part // LANES
+
+    def product(base, g):
+        rows = slice(g * group * chunk, (g + 1) * group * chunk)
+        s = sk_hl[:, rows]
+        acc = None
+        for whole in (khi, klo):
+            block = jnp.concatenate([whole[base + i, rows, :] for i in range(tiles)], axis=1)
+            term = lax.dot_general(s, block, NN, preferred_element_type=F32)
+            acc = term if acc is None else acc + term
+        return acc[:rank] + acc[rank:]
+
+    def take(g):
+        if C > 1:
+            all_received(sk_all.at[pl.ds(0, C - 1), pl.ds(0, group)], sk_rs.at[g])
+        pieces = []
+        for rc in range(g * group, (g + 1) * group):
+            total = sk_all[0, rc]
+            for c in range(1, C):
+                total = total + sk_all[c, rc]
+            pieces.append(total)
+        sketch = jnp.concatenate(pieces, axis=1)
+        high, low = split(0.25 * sketch)
+        rows = slice(g * group * chunk, (g + 1) * group * chunk)
+        sk_hl[0:rank, rows] = high
+        sk_hl[rank : 2 * rank, rows] = low
+        return sketch, lax.dot_general(sketch, sketch, NT, precision=HIGHEST, preferred_element_type=F32)
+
+    parts, gram = [], None
+    for g in range(groups):
+        some, term = take(g)
+        parts.append(some)
+        gram = term if gram is None else gram + term
+        if g == groups - 1:
+            break
+
+        def early(b, carry):
+            acc = product(b * tiles, g)
+            if g > 0:
+                acc = acc + wacc[b]
+            wacc[b] = acc
+            return carry
+
+        loop(0, half, early)
+    sketch = jnp.concatenate(parts, axis=1)
     g_src[...] = jnp.zeros_like(g_src)
-    g_src[:, rank : 2 * rank] = gram
+    g_src[:, rank : 2 * rank] = gram / rows_total
     g_all[me] = g_src[...]
 
     def gram_copy(t):
-        return remote(g_src, g_all.at[me], g_ss.at[t], g_rs.at[t], "row", row_of(t))
+        return remote(g_src, g_all.at[me], g_ss, g_rs, "row", row_of(t))
 
     for t in range(1, R):
         gram_copy(t).start()
 
     def pair_copy(t):
-        return remote(wp.at[t, 1 - side], s_in.at[t], p_ss.at[t], p_rs.at[t], "row", sib)
+        return remote(wp.at[t, 1 - side], s_in.at[t], p_ss, p_rs.at[t], "row", sib)
 
     def w_copy(t):
-        return remote(w_src.at[t], w_all.at[t], w_ss.at[t], w_rs.at[t], "row", 2 * chip_to(t) + side)
-
-    tiles = 2 * part // LANES
-
-    def product(t):
-        base = chip_to(t) * tiles
-        s = sk_hl[...]
-        acc = None
-        for whole in (khi, klo):
-            block = jnp.concatenate([whole[base + i] for i in range(tiles)], axis=1)
-            term = lax.dot_general(s, block, NN, preferred_element_type=F32)
-            acc = term if acc is None else acc + term
-        acc = acc[:rank] + acc[rank:]
+        return remote(w_src.at[t], w_all.at[t], w_ss, w_rs, "row", 2 * chip_to(t) + side)
+
+    def blocks(t):
+        to = chip_to(t)
+        acc = product(to * tiles, groups - 1)
+        if groups > 1:
+            acc = acc + wacc[to]
         wp[t, 0] = acc[:, :part]
         wp[t, 1] = acc[:, part:]
 
@@ -226,14 +276,16 @@
 
     before = None
     for t in far_first:
-        product(t)
+        blocks(t)
         pair_copy(t).start()
         if before is not None:
             forward(before)
         before = t
-    for t in range(1, R):
-        gram_copy(t).wait_recv()
-    product(0)
+    blocks(0)
+    pair_copy(0).start()
+    if before is not None:
+        forward(before)
+    all_received(g_all.at[pl.ds(0, R - 1)], g_rs)
     mat = g_all[0]
     for r in range(1, R):
         mat = mat + g_all[r]
@@ -247,77 +299,81 @@
     diag = jnp.sum(jnp.where(lane == sub + rank, mat, 0.0), axis=1, keepdims=True)
     inverse = (mat * (1.0 / jnp.sqrt(diag)))[:, :rank]
     inverse = jnp.where(lane[:, :rank] <= sub[:, :rank], inverse, 0.0)
-    pair_copy(0).start()
-    if before is not None:
-        forward(before)
     basis_ref[...] = jnp.dot(inverse, sketch, precision=HIGHEST, preferred_element_type=F32)
     pair_copy(0).wait_recv()
     total = wp[0, side] + s_in[0]
+    if half > 1:
+        all_received(w_all.at[pl.ds(0, half - 1)], w_rs)
     for t in far_first:
-        w_copy(t).wait_recv()
         total = total + w_all[t]
     mine = jnp.dot(inverse, total, precision=HIGHEST, preferred_element_type=F32)
     img[me] = mine
 
     def far_copy(t):
-        return remote(img.at[me], img.at[me], a_ss.at[t], a_rs.at[t], "row", 2 * chip_to(t) + side)
+        return remote(img.at[me], img.at[me], a_ss, a_rs.at[t], "row", 2 * chip_to(t) + side)
 
     def near_copy(t):
         slot = 2 * chip_from(t) + side
-        return remote(img.at[slot], img.at[slot], f_ss.at[t], f_rs.at[t], "row", sib)
-
-    def core_copy(t):
-        return remote(c_src, c_all.at[me], c_ss.at[t], c_rs.at[t], "row", row_of(t))
-
-    def last_copy(t):
-        return remote(d_src, d_all.at[mc], d_ss.at[t], d_rs.at[t], "col", lax.rem(mc + t, C))
-
-    core = lax.dot_general(mine, mine, NT, precision=HIGHEST, preferred_element_type=F32) / order
-    c_src[...] = jnp.zeros_like(c_src)
-    c_src[:, 0:rank] = core
-    c_all[me] = c_src[...]
-    for t in range(1, R):
-        core_copy(t).start()
+        return remote(img.at[slot], img.at[slot], f_ss, f_rs, "row", sib)
+
+    def core_copy(k):
+        return pltpu.make_async_remote_copy(
+            src_ref=c_src, dst_ref=c_all.at[index], send_sem=c_ss, recv_sem=c_rs,
+            device_id=peer(k), device_id_type=pl.DeviceIdType.MESH,
+        )
+
+    per_row = LANES // rank
+    packed = rank // per_row
+    sub = lax.broadcasted_iota(jnp.int32, (rank, LANES), 0)
+    lane = lax.broadcasted_iota(jnp.int32, (rank, LANES), 1)
+    own = lane // rank == lax.rem(sub, per_row)
+
+    both = jnp.concatenate(split(mine), axis=0)
+    core = lax.dot_general(both, both, NT, preferred_element_type=F32) / order
+    core = core[:rank] + core[rank:]
+    core = core[:, :rank] + core[:, rank:]
+    wide = jnp.where(own, jnp.concatenate([core] * per_row, axis=1), 0.0)
+    flat = jnp.concatenate(
+        [jnp.sum(wide[a * per_row : (a + 1) * per_row, :], axis=0, keepdims=True) for a in range(packed)], axis=0
+    )
+    c_src[...] = flat
+    c_all[index] = flat
+
+    def send_core(k, carry):
+        core_copy(k).start()
+        return carry
+
+    loop(1, devices, send_core)
     for t in far_first:
         far_copy(t).start()
     near_copy(0).start()
-    for t in range(1, R):
-        core_copy(t).wait_recv()
-    core = c_all[0]
-    for r in range(1, R):
-        core = core + c_all[r]
-    d_src[...] = core
-    d_all[mc] = core
-    for t in range(1, C):
-        last_copy(t).start()
     for t in reversed(far_first):
         far_copy(t).wait_recv()
         near_copy(t).start()
-    for t in range(half):
-        near_copy(t).wait_recv()
+    all_received(img.at[pl.ds(0, half)], f_rs)
     for r in range(R):
         image_ref[:, r * part : (r + 1) * part] = img[r]
-    for t in range(1, C):
-        last_copy(t).wait_recv()
-    core = d_all[0]
-    for c in range(1, C):
-        core = core + d_all[c]
-    core_ref[...] = core[:, 0:rank]
-
-    for rc in range(chunks):
-        for t in range(1, C):
-            sketch_copy(rc, t).wait_send()
-    for t in range(1, R):
-        gram_copy(t).wait_send()
-        core_copy(t).wait_send()
-    for t in range(half):
-        pair_copy(t).wait_send()
-        near_copy(t).wait_send()
-    for t in far_first:
-        w_copy(t).wait_send()
-        far_copy(t).wait_send()
-    for t in range(1, C):
-        last_copy(t).wait_send()
+    all_received(c_all.at[pl.ds(0, devices - 1)], c_rs)
+    flat = jnp.sum(c_all[...], axis=0)
+    wide = jnp.concatenate(
+        [jnp.broadcast_to(flat[a : a + 1, :], (per_row, LANES)) for a in range(packed)], axis=0
+    )
+    wide = jnp.where(own, wide, 0.0)
+    shift = LANES // 2
+    while shift >= rank:
+        wide = wide + pltpu.roll(wide, shift, 1)
+        shift //= 2
+    core_ref[...] = wide[:, 0:rank]
+
+    if C > 1:
+        all_sent(sk_all.at[pl.ds(0, C - 1)], sk_ss)
+    all_sent(g_all.at[pl.ds(0, R - 1)], g_ss)
+    all_sent(s_in, p_ss)
+    if half > 1:
+        all_sent(w_all.at[pl.ds(0, half - 1)], w_ss)
+        all_sent(img.at[pl.ds(0, half - 1)], a_ss)
+    all_sent(img.at[pl.ds(0, half)], f_ss)
+    all_sent(c_all.at[pl.ds(0, devices - 1)], c_ss)
 
 
 def finish(*refs):
@@ -334,6 +390,7 @@
     M, N = row_cells.shape[1], col_cells.shape[1]
     chunk = min(M, UNIT)
     chunks, part, half = M // chunk, N // R, R // 2
+    groups = chunks // max(chunks // 2, 1)
     shape = (R, C, rank, M, N, M * R, N * C)
     vmem = pltpu.VMEM
     dma = pltpu.SemaphoreType.DMA
@@ -365,29 +422,20 @@
             vmem((2 * rank, M), BF16),
             vmem((rank, LANES), F32),
             vmem((R, rank, LANES), F32),
+            vmem((half, rank, 2 * part), F32),
             vmem((half, 2, rank, part), F32),
             vmem((half, rank, part), F32),
             vmem((half, rank, part), F32),
             vmem((half, rank, part), F32),
             vmem((R, rank, part), F32),
-            vmem((rank, LANES), F32),
-            vmem((R, rank, LANES), F32),
-            vmem((rank, LANES), F32),
-            vmem((C, rank, LANES), F32),
-            dma((3,)),
-            dma((chunks, C)), dma((chunks, C)),
-            dma((R,)), dma((R,)),
-            dma((half,)), dma((half,)),
-            dma((half,)), dma((half,)),
-            dma((half,)), dma((half,)),
-            dma((half,)), dma((half,)),
-            dma((R,)), dma((R,)),
-            dma((C,)), dma((C,)),
+            vmem((rank * rank // LANES, LANES), F32),
+            vmem((R * C, rank * rank // LANES, LANES), F32),
+            dma((3,)), dma((groups,)), dma((half,)), dma((half,)), dma((11,)),
         ],
         compiler_params=pltpu.CompilerParams(
-            collective_id=0, has_side_effects=True, vmem_limit_bytes=48 * 1024 * 1024
+            collective_id=0, has_side_effects=True, vmem_limit_bytes=VMEM_LIMIT
         ),
-    )(row_cells, col_cells, omega)
+    )(*(pltpu.with_memory_space_constraint(x, pltpu.HBM) for x in (row_cells, col_cells, omega)))
     return pl.pallas_call(
         finish,
         out_shape=out_shape,

time: 44.2 us -> 39.8 us (0.900)
  local copies, waits for them, and re-layouts: 2.66 us -> 0 us
  Pallas kernels: 40.7 us -> 39 us
    unnamed x6 -> x0, local copies, waits for them, and re-layouts: 2.66 us -> none
    pallas_call x1, Pallas kernels: 39.8 us -> 38.1 us  [shards(): pl.pallas_call(functools.partial(kernel, shape), out_shape=out_shape, in_...]
where the time goes in v2:
time: 39.8 us; the launch traced here: 39.6 us
  Pallas kernels  39 us (98%)
  between operations  0.64 us (2%)
    pallas_call x1, Pallas kernels, shards(): pl.pallas_call(functools.partial(kernel, shape), out_shape=out_shape, in_...  38.1 us
    pallas_call x1, Pallas kernels, shards(): pl.pallas_call(finish, out_shape=out_shape, in_specs=[full] * 3, out_spec...  0.85 us

profile of v2, /device:TPU:0, one launch (start us, length us, event | category | flops | bytes accessed | tf_op | source)
XLA Modules:
  0.0 39.6 jit_solution(16729216781460346113)
XLA Ops:
  0.6 38.1 %shard_map.58 = (f32[16,1024]{1,0:T(8,128)S(1)}, f32[16,8192]{1,0:T(8,128)S(1)}, f32[16,16]{1,0:T(8,128)S(1)}) custom-call(s32[3,1024]{1,0:T(4,128)} %row_hbm.1, s32[3,8192]{1,0:T(4,128)} %col_hbm.1, f32[16,8192]{1,0:T(8,128)} %omega_hbm.1), custom_call_target="tpu_custom_call" | custom-call | tf_op jit(solution)/shard_map/pallas_call | solution.py:404
  38.8 0.8 %shard_map.59 = (f32[16,1024]{1,0:T(8,128)}, f32[16,8192]{1,0:T(8,128)}, f32[16,16]{1,0:T(8,128)}) custom-call(f32[16,1024]{1,0:T(8,128)S(1)} %get-tuple-element.6.refs_0_, f32[16,8192]{1,0:T(8,128)S(1)} %get-tuple-element.7.refs_1_, f32[16,16]{1,0:T(8,128)S(1)} %get-tuple-element.8.refs_2_), custom_call_target="tpu_custom_call" | custom-call | tf_op jit(solution)/shard_map/pallas_call | solution.py:439
